TPU v7x, 32 devices: a whole 2x2x4 slice. The times are simulated.
32 devices in a mesh: shard: 2 (over core), ctx: 4 (over y, x), tp: 4 (over z).
Axes of the slice: x: 2, y: 2, z: 4, core: 2. Of those that a mesh axis runs over, the one named last changes fastest.
Arguments:
- tokens: bfloat16 [2, 4096, 1024], P('shard', 'ctx'), may hold values from -6 to 6
- lengths: int32 [2], P('shard'), may hold values from 1024 to 4096, as said below
- routes: int32 [2, 4096, 1], P('shard', 'ctx'), may hold values from 0 to 7; in each aligned block of 1024 rows (0 to 1023, 1024 to 2047, ..., all dimensions but the last counted through in order) at most 384 rows name the same one
- priority: int32 [2, 4096], P('shard', 'ctx'), may hold values from 0 to 8191, as said below
- attn_gain: bfloat16 [1024], P(('shard', 'ctx')), may hold values from 0.5 to 1.5
- qkv_weight: bfloat16 [1024, 3, 1024], P(('shard', 'ctx'), None, 'tp'), may hold values from -0.1875 to 0.1875
- proj_weight: bfloat16 [1024, 1024], P('tp', ('shard', 'ctx')), may hold values from -2 to 2
- ffn_gain: bfloat16 [1024], P(('shard', 'ctx')), may hold values from 0.5 to 1.5
- mix_weight: bfloat16 [1024, 2], P(('shard', 'ctx')), may hold values from -0.1875 to 0.1875
- up_weight: bfloat16 [1024, 4096], P(('shard', 'ctx'), 'tp'), may hold values from -0.1875 to 0.1875
- down_weight: bfloat16 [4096, 1024], P('tp', ('shard', 'ctx')), may hold values from -0.09375 to 0.09375
- expert_up: bfloat16 [8, 1024, 4096], P(('shard', 'ctx'), None, 'tp'), may hold values from -0.1875 to 0.1875
- expert_down: bfloat16 [8, 4096, 1024], P(('shard', 'ctx'), 'tp'), may hold values from -0.09375 to 0.09375
- cotangent: bfloat16 [2, 4096, 1024], P('shard', 'ctx'), may hold values from -6 to 6
Outputs:
- layer_out: bfloat16 [2, 4096, 1024], P('shard', 'ctx')
- tokens_grad: bfloat16 [2, 4096, 1024], P('shard', 'ctx')
- attn_gain_grad: float32 [1024], P(('shard', 'ctx'))
- qkv_weight_grad: float32 [1024, 3, 1024], P(('shard', 'ctx'), None, 'tp')
- proj_weight_grad: float32 [1024, 1024], P('tp', ('shard', 'ctx'))
- ffn_gain_grad: float32 [1024], P(('shard', 'ctx'))
- mix_weight_grad: float32 [1024, 2], P(('shard', 'ctx'))
- up_weight_grad: float32 [1024, 4096], P(('shard', 'ctx'), 'tp')
- down_weight_grad: float32 [4096, 1024], P('tp', ('shard', 'ctx'))
- expert_up_grad: float32 [8, 1024, 4096], P(('shard', 'ctx'), None, 'tp')
- expert_down_grad: float32 [8, 4096, 1024], P(('shard', 'ctx'), 'tp')
Inputs may be any that keep to these rules, and one draw needn't show every extreme that they name: `lengths`: padding positions are those at or past a slot's length; some slot has exactly 4096 live positions. `routes`: in the rows of one device (one slot's 1024 positions on one index of ctx), at most 384 positions name the same expert, and exactly 384 do for some expert on some device. `priority`: each value 0 to 8191 occurs at exactly one position of all slots.
All inputs are finite; a program needn't handle non-finite values.
Results may differ from a plain program's by a relative error of at most 0.024.
Values may be sent and summed in bfloat16 or wider, within the bound.
A program may use at most 192 MiB of HBM per device.

v0:
```python
import jax
import jax.numpy as jnp
from jax import lax
from jax.sharding import PartitionSpec as P

HD = 64
CAP = 1152
empty_mark = 1 << 30
norm_eps = 1e-05
masked_score = -1e30


def gelu_tanh(values):
    return jax.nn.gelu(values, approximate=True)


def norm_forward(values, gain_vec):
    average = jnp.mean(values, axis=-1, keepdims=True)
    centred = values - average
    spread = jnp.mean(centred * centred, axis=-1, keepdims=True)
    inverse = lax.rsqrt(spread + norm_eps)
    unit_rows = centred * inverse
    return (unit_rows * gain_vec, unit_rows, inverse)


def norm_backward(upstream, gain_vec, unit_rows, inverse):
    shaped = upstream * gain_vec
    first_term = jnp.mean(shaped, axis=-1, keepdims=True)
    second_term = jnp.mean(shaped * unit_rows, axis=-1, keepdims=True)
    return (
        inverse * (shaped - first_term - unit_rows * second_term),
        jnp.sum(upstream * unit_rows, axis=0),
    )


def local(
    tokens,
    lengths,
    routes,
    priority,
    attn_gain,
    qkv_weight,
    proj_weight,
    ffn_gain,
    mix_weight,
    up_weight,
    down_weight,
    expert_up,
    expert_down,
    cotangent,
):
    seq_dev = tokens.shape[1]
    model_width = tokens.shape[2]
    full_len = seq_dev * lax.axis_size("ctx")
    positions = lax.axis_index("ctx") * seq_dev + jnp.arange(seq_dev, dtype=jnp.int32)
    live_mask = positions < lengths[0]
    live_rows = live_mask.astype(jnp.float32)[:, None]
    inputs = tokens[0].astype(jnp.float32)
    gain_one, qkv_full, proj_full, gain_two, mix_full, up_full, down_full = (
        lax.all_gather(attn_gain, ("shard", "ctx"), axis=0, tiled=True),
        lax.all_gather(qkv_weight, ("shard", "ctx"), axis=0, tiled=True),
        lax.all_gather(proj_weight, ("shard", "ctx"), axis=1, tiled=True),
        lax.all_gather(ffn_gain, ("shard", "ctx"), axis=0, tiled=True),
        lax.all_gather(mix_weight, ("shard", "ctx"), axis=0, tiled=True),
        lax.all_gather(up_weight, ("shard", "ctx"), axis=0, tiled=True),
        lax.all_gather(down_weight, ("shard", "ctx"), axis=1, tiled=True),
    )
    gain_one = gain_one.astype(jnp.float32)
    gain_two = gain_two.astype(jnp.float32)
    local_heads = qkv_full.shape[2] // HD
    score_scale = HD ** (-0.5)
    normed, unit_one, inverse_one = norm_forward(inputs, gain_one)
    normed_low = normed.astype(jnp.bfloat16)
    projected = jnp.einsum(
        "td,dcf->tcf", normed_low, qkv_full, preferred_element_type=jnp.float32
    ).astype(jnp.bfloat16)
    queries = projected[:, 0].reshape(seq_dev, local_heads, HD)
    keys_all, values_all = (
        lax.all_gather(projected[:, 1], "ctx", axis=0, tiled=True),
        lax.all_gather(projected[:, 2], "ctx", axis=0, tiled=True),
    )
    key_block = min(full_len, 1024)
    block_count = full_len // key_block
    key_blocks = keys_all.reshape(block_count, key_block, local_heads, HD)
    value_blocks = values_all.reshape(block_count, key_block, local_heads, HD)
    key_places = jnp.arange(full_len, dtype=jnp.int32).reshape(block_count, key_block)

    def allowed(places):
        return ((places[None, :] <= positions[:, None]) & (places[None, :] < lengths[0]))[None]

    def forward_step(state_now, pieces):
        running_max, running_sum, weighted = state_now
        key_rows, value_rows, places = pieces
        visible = allowed(places)
        scores = (
            jnp.einsum("qhd,khd->hqk", queries, key_rows, preferred_element_type=jnp.float32)
            * score_scale
        )
        scores = jnp.where(visible, scores, masked_score)
        new_max = jnp.maximum(running_max, jnp.max(scores, axis=-1))
        weights = jnp.where(visible, jnp.exp(scores - new_max[..., None]), 0.0)
        shrink = jnp.exp(running_max - new_max)
        running_sum = running_sum * shrink + jnp.sum(weights, axis=-1)
        weighted = weighted * shrink[..., None] + jnp.einsum(
            "hqk,khd->hqd",
            weights.astype(jnp.bfloat16),
            value_rows,
            preferred_element_type=jnp.float32,
        )
        return ((new_max, running_sum, weighted), None)

    start_state = (
        jnp.full((local_heads, seq_dev), masked_score, jnp.float32),
        jnp.zeros((local_heads, seq_dev), jnp.float32),
        jnp.zeros((local_heads, seq_dev, HD), jnp.float32),
    )
    (running_max, running_sum, weighted), _ = lax.scan(
        forward_step, start_state, (key_blocks, value_blocks, key_places)
    )
    log_total = running_max + jnp.log(running_sum)
    heads_out = weighted / running_sum[..., None]
    attended_low = jnp.transpose(heads_out, (1, 0, 2)).reshape(seq_dev, -1).astype(jnp.bfloat16)
    branch_part = jnp.dot(attended_low, proj_full, preferred_element_type=jnp.float32)
    branch = lax.psum(branch_part.astype(jnp.bfloat16), "tp").astype(jnp.float32)
    middle = inputs + branch
    normed2, unit_two, inverse_two = norm_forward(middle, gain_two)
    normed2_low = normed2.astype(jnp.bfloat16)
    mixing = jax.nn.softmax(
        jnp.dot(normed2_low, mix_full, preferred_element_type=jnp.float32), axis=-1
    )
    upper_pre = jnp.dot(normed2_low, up_full, preferred_element_type=jnp.float32)
    hidden_low = gelu_tanh(upper_pre).astype(jnp.bfloat16)
    dense_part = jnp.dot(hidden_low, down_full, preferred_element_type=jnp.float32)
    experts_total = lax.axis_size(("shard", "ctx"))
    slot_cap = max(4, 3 * seq_dev // experts_total)
    chosen = routes[0, :, 0]
    onehot = (chosen[:, None] == jnp.arange(experts_total, dtype=jnp.int32)[None, :]).astype(
        jnp.int32
    )
    slot_pos = jnp.sum(jnp.cumsum(onehot, axis=0) * onehot, axis=1) - 1
    target = jnp.where(live_mask, chosen * slot_cap + slot_pos, experts_total * slot_cap)

    def pack_rows(token_rows):
        buffer = jnp.zeros((experts_total * slot_cap, model_width), token_rows.dtype)
        return (
            buffer.at[target]
            .set(token_rows, mode="drop")
            .reshape(experts_total, slot_cap, model_width)
        )

    send_order = (
        jnp.full((experts_total * slot_cap,), empty_mark, jnp.int32)
        .at[target]
        .set(priority[0], mode="drop")
    )
    recv_rows, recv_order = (
        lax.all_to_all(
            pack_rows(normed2_low), ("shard", "ctx"), split_axis=0, concat_axis=0, tiled=True
        ),
        lax.all_to_all(
            send_order.reshape(experts_total, slot_cap),
            ("shard", "ctx"),
            split_axis=0,
            concat_axis=0,
            tiled=True,
        ),
    )
    flat_order = recv_order.reshape(-1)
    ranking = jnp.argsort(flat_order)[:CAP]
    taken_mask = (flat_order[ranking] < empty_mark).astype(jnp.float32)[:, None]
    expert_in = recv_rows.reshape(-1, model_width)[ranking]
    own_up = expert_up[0]
    own_down = expert_down[0]
    expert_pre = jnp.dot(expert_in, own_up, preferred_element_type=jnp.float32)
    expert_hidden = gelu_tanh(expert_pre).astype(jnp.bfloat16)
    expert_part = jnp.dot(expert_hidden, own_down, preferred_element_type=jnp.float32) * taken_mask

    def unfold_rows(slot_rows):
        buffer = jnp.zeros((experts_total * slot_cap, model_width), jnp.float32)
        return buffer.at[ranking].set(slot_rows).reshape(experts_total, slot_cap, model_width)

    full_index = jnp.where(live_mask, chosen * slot_cap + slot_pos, 0)
    returned_rows = lax.all_to_all(
        unfold_rows(expert_part).astype(jnp.bfloat16),
        ("shard", "ctx"),
        split_axis=0,
        concat_axis=0,
        tiled=True,
    ).astype(jnp.float32)
    expert_tok = returned_rows.reshape(-1, model_width)[full_index] * live_rows
    mixed_part = mixing[:, 0:1] * dense_part + mixing[:, 1:2] * expert_tok
    mixed = lax.psum(mixed_part.astype(jnp.bfloat16), "tp").astype(jnp.float32)
    layer_out = ((middle + mixed) * live_rows).astype(jnp.bfloat16)[None]
    out_grad = cotangent[0].astype(jnp.float32) * live_rows
    dense_grad = (mixing[:, 0:1] * out_grad).astype(jnp.bfloat16)
    expert_grad = (mixing[:, 1:2] * out_grad).astype(jnp.bfloat16)
    dots_part = jnp.stack(
        [jnp.sum(out_grad * dense_part, axis=-1), jnp.sum(out_grad * expert_tok, axis=-1)], axis=-1
    )
    down_grad = jnp.einsum("tf,td->fd", hidden_low, dense_grad, preferred_element_type=jnp.float32)
    hidden_grad = jnp.einsum("td,fd->tf", dense_grad, down_full, preferred_element_type=jnp.float32)
    _, gelu_pull = jax.vjp(gelu_tanh, upper_pre)
    upper_grad = gelu_pull(hidden_grad)[0].astype(jnp.bfloat16)
    up_grad = jnp.einsum("td,tf->df", normed2_low, upper_grad, preferred_element_type=jnp.float32)
    normed2_part = jnp.einsum("tf,df->td", upper_grad, up_full, preferred_element_type=jnp.float32)
    recv_grad = lax.all_to_all(
        pack_rows(expert_grad), ("shard", "ctx"), split_axis=0, concat_axis=0, tiled=True
    )
    grad_in = recv_grad.reshape(-1, model_width)[ranking]
    own_down_grad = jnp.einsum(
        "cf,cd->fd", expert_hidden, grad_in, preferred_element_type=jnp.float32
    )
    ehidden_grad = jnp.einsum("cd,fd->cf", grad_in, own_down, preferred_element_type=jnp.float32)
    _, expert_pull = jax.vjp(gelu_tanh, expert_pre)
    epre_grad = expert_pull(ehidden_grad)[0].astype(jnp.bfloat16)
    own_up_grad = jnp.einsum("cd,cf->df", expert_in, epre_grad, preferred_element_type=jnp.float32)
    expert_in_grad = jnp.einsum("cf,df->cd", epre_grad, own_up, preferred_element_type=jnp.float32)
    sent_back = lax.all_to_all(
        unfold_rows(expert_in_grad).astype(jnp.bfloat16),
        ("shard", "ctx"),
        split_axis=0,
        concat_axis=0,
        tiled=True,
    ).astype(jnp.float32)
    expert_tok_grad = sent_back.reshape(-1, model_width)[full_index] * live_rows
    normed2_grad, branch_dots = (
        lax.psum((normed2_part + expert_tok_grad).astype(jnp.bfloat16), "tp").astype(jnp.float32),
        lax.psum(dots_part.astype(jnp.bfloat16), "tp").astype(jnp.float32),
    )
    logit_grad = mixing * (branch_dots - jnp.sum(mixing * branch_dots, axis=-1, keepdims=True))
    mix_grad = jnp.dot(
        normed2_low.astype(jnp.float32).T, logit_grad, precision=lax.Precision.HIGHEST
    )
    normed2_grad = normed2_grad + jnp.dot(
        logit_grad, mix_full.astype(jnp.float32).T, precision=lax.Precision.HIGHEST
    )
    middle_norm_grad, gain_two_grad = norm_backward(normed2_grad, gain_two, unit_two, inverse_two)
    middle_grad = out_grad + middle_norm_grad
    branch_grad = middle_grad.astype(jnp.bfloat16)
    proj_grad = jnp.einsum(
        "tf,td->fd", attended_low, branch_grad, preferred_element_type=jnp.float32
    )
    attended_grad = jnp.einsum(
        "td,fd->tf", branch_grad, proj_full, preferred_element_type=jnp.float32
    ).astype(jnp.bfloat16)
    grad_heads = attended_grad.reshape(seq_dev, local_heads, HD)
    row_delta = jnp.sum(
        jnp.transpose(grad_heads, (1, 0, 2)).astype(jnp.float32) * heads_out, axis=-1
    )

    def backward_step(query_grad, pieces):
        key_rows, value_rows, places = pieces
        visible = allowed(places)
        scores = (
            jnp.einsum("qhd,khd->hqk", queries, key_rows, preferred_element_type=jnp.float32)
            * score_scale
        )
        probs = jnp.where(visible, jnp.exp(scores - log_total[..., None]), 0.0)
        prob_grad = jnp.einsum(
            "qhd,khd->hqk", grad_heads, value_rows, preferred_element_type=jnp.float32
        )
        score_grad = (probs * (prob_grad - row_delta[..., None])).astype(jnp.bfloat16)
        query_grad = query_grad + jnp.einsum(
            "hqk,khd->qhd", score_grad, key_rows, preferred_element_type=jnp.float32
        )
        key_grad = jnp.einsum(
            "hqk,qhd->khd", score_grad, queries, preferred_element_type=jnp.float32
        )
        value_grad = jnp.einsum(
            "hqk,qhd->khd",
            probs.astype(jnp.bfloat16),
            grad_heads,
            preferred_element_type=jnp.float32,
        )
        return (query_grad, (key_grad, value_grad))

    query_grad, (key_grad_blocks, value_grad_blocks) = lax.scan(
        backward_step,
        jnp.zeros((seq_dev, local_heads, HD), jnp.float32),
        (key_blocks, value_blocks, key_places),
    )
    key_grad_all = key_grad_blocks.reshape(full_len, -1) * score_scale
    value_grad_all = value_grad_blocks.reshape(full_len, -1)
    key_grad_own, value_grad_own = (
        lax.psum_scatter(
            key_grad_all.astype(jnp.bfloat16), "ctx", scatter_dimension=0, tiled=True
        ).astype(jnp.float32),
        lax.psum_scatter(
            value_grad_all.astype(jnp.bfloat16), "ctx", scatter_dimension=0, tiled=True
        ).astype(jnp.float32),
    )
    qkv_grad = jnp.stack(
        [(query_grad * score_scale).reshape(seq_dev, -1), key_grad_own, value_grad_own], axis=1
    ).astype(jnp.bfloat16)
    qkv_grad_full = jnp.einsum(
        "td,tcf->dcf", normed_low, qkv_grad, preferred_element_type=jnp.float32
    )
    normed_part = jnp.einsum("tcf,dcf->td", qkv_grad, qkv_full, preferred_element_type=jnp.float32)
    normed_grad = lax.psum(normed_part.astype(jnp.bfloat16), "tp").astype(jnp.float32)
    input_norm_grad, gain_one_grad = norm_backward(normed_grad, gain_one, unit_one, inverse_one)
    tokens_grad = (middle_grad + input_norm_grad).astype(jnp.bfloat16)[None]
    shares = (
        lax.psum_scatter(gain_one_grad, ("shard", "ctx"), scatter_dimension=0, tiled=True),
        lax.psum_scatter(qkv_grad_full, ("shard", "ctx"), scatter_dimension=0, tiled=True),
        lax.psum_scatter(proj_grad, ("shard", "ctx"), scatter_dimension=1, tiled=True),
        lax.psum_scatter(gain_two_grad, ("shard", "ctx"), scatter_dimension=0, tiled=True),
        lax.psum_scatter(mix_grad, ("shard", "ctx"), scatter_dimension=0, tiled=True),
        lax.psum_scatter(up_grad, ("shard", "ctx"), scatter_dimension=0, tiled=True),
        lax.psum_scatter(down_grad, ("shard", "ctx"), scatter_dimension=1, tiled=True),
    )
    return (
        layer_out,
        tokens_grad,
        shares[0],
        shares[1],
        shares[2],
        shares[3],
        shares[4],
        shares[5],
        shares[6],
        own_up_grad[None],
        own_down_grad[None],
    )


def solution(mesh):
    placed = (
        P("shard", "ctx", None),
        P("shard"),
        P("shard", "ctx", None),
        P("shard", "ctx"),
        P(("shard", "ctx")),
        P(("shard", "ctx"), None, "tp"),
        P("tp", ("shard", "ctx")),
        P(("shard", "ctx")),
        P(("shard", "ctx"), None),
        P(("shard", "ctx"), "tp"),
        P("tp", ("shard", "ctx")),
        P(("shard", "ctx"), None, "tp"),
        P(("shard", "ctx"), "tp", None),
        P("shard", "ctx", None),
    )
    return jax.shard_map(
        local,
        mesh=mesh,
        in_specs=placed,
        out_specs=(
            P("shard", "ctx", None),
            P("shard", "ctx", None),
            P(("shard", "ctx")),
            P(("shard", "ctx"), None, "tp"),
            P("tp", ("shard", "ctx")),
            P(("shard", "ctx")),
            P(("shard", "ctx"), None),
            P(("shard", "ctx"), "tp"),
            P("tp", ("shard", "ctx")),
            P(("shard", "ctx"), None, "tp"),
            P(("shard", "ctx"), "tp", None),
        ),
        check_vma=False,
    )
```

profile of v0, /device:TPU:0, one launch (start us, length us, event | category | flops | bytes accessed | tf_op | source)
XLA Modules:
  0.0 1538.6 jit_solution(16928028134594946048)
XLA Ops:
  9.2 15.0 all-gather.2
  28.5 10.5 all-gather.10.cloned.1.call-done
  45.0 24.4 %all_gather.31 = bf16[256,1024]{1,0:T(8,128)(2,1)S(1)} all-gather(bf16[256,128]{1,0:T(8,128)(2,1)S(1)} %copy-done.32), channel_id=1, replica_groups=mesh['shard'=2,'ctx'=4,'tp'=4] {'shard','ctx'}, dimensions={1}, use_global_device_ids=true | all-gather | bytes 589824 | tf_op jit(solution)/shard_map/all_gather | solution.py:62
  69.4 13.8 all-gather.18.cloned.1.call-done
  91.3 29.6 %all-gather.16.cloned.1.call-done = bf16[4096,1,256]{0,2,1:T(8,128)(2,1)} async-done(((bf16[1024,1,256]{0,2,1:T(8,128)(2,1)}), bf16[4096,1,256]{0,2,1:T(8,128)(2,1)}) %all-gather.16.cloned.1.call-update) | async-done | bytes 2097168 | tf_op jit(solution)/shard_map/all_gather | solution.py:79
  128.9 67.9 %while.30 = (s32[]{:T(128)}, f32[4,1024]{1,0:T(4,128)S(1)}, f32[4,1024]{1,0:T(4,128)S(1)}, f32[4,1024,64]{1,2,0:T(8,128)}, s32[4,1024]{1,0:T(4,128)S(1)}, /*inde...) while((s32[]{:T(128)}, f32[4,1024]{1,0:T(4,128)S(1)}, ...), condition=%wide.region_5.6_spmd.clone, body=%wide.region_2.5_spmd.clone.sunk | while | flops 1131173888 | bytes 66869456 | solution.py:117
  213.3 14.5 all-gather.3
  227.8 59.8 %all-reduce.8.cloned.1.call-done = bf16[1024,1024]{1,0:T(8,128)(2,1)} async-done(((bf16[1024,1024]{1,0:T(8,128)(2,1)}), bf16[1024,1024]{1,0:T(8,128)(2,1)}) %all-reduce.8.cloned.1.call-update) | async-done | bytes 2097168 | tf_op jit(solution)/shard_map/psum | solution.py:124
  294.8 9.8 scatter_custom_fusion.1
  322.2 66.5 %all-to-all-done.1 = bf16[8,384,1024]{2,1,0:T(8,128)(2,1)} async-done(((bf16[8,384,1024]{2,1,0:T(8,128)(2,1)}), bf16[8,384,1024]{2,1,0:T(8,128)(2,1)}, u32[]{:S(2)}, u32[]{:S(2)}) %all-to-all-start.1) | async-done | bytes 6291488 | tf_op jit(solution)/shard_map/all_to_all | solution.py:157
  388.8 10.2 gather_fusion
  410.7 14.5 scatter_custom_fusion.2
  425.2 8.2 convert_element_type.175
  438.9 86.6 %all_gather.33 = bf16[1024,2]{0,1:T(2,128)(2,1)S(1)} all-gather(bf16[128,2]{0,1:T(2,128)(2,1)S(1)} %copy-done.54), channel_id=1, replica_groups=mesh['shard'=2,'ctx'=4,'tp'=4] {'shard','ctx'}, dimensions={0}, use_global_device_ids=true | all-gather | bytes 4608 | tf_op jit(solution)/shard_map/all_gather | solution.py:64
  534.3 8.9 bitcast_convert_fusion.1
  543.2 10.9 gather_fusion.2
  554.1 9.6 fusion.91
  563.7 10.0 psum.38
  573.8 10.1 scatter_custom_fusion.3
  583.9 76.7 %all_to_all.29 = bf16[8,384,1024]{2,1,0:T(8,128)(2,1)} all-to-all(bf16[8,384,1024]{2,1,0:T(8,128)(2,1)} %bitcast.322), channel_id=1, replica_groups=mesh['shard'=2,'ctx'=4,'tp'=4] {'shard','ctx'}, dimensions={0} | all-to-all | bytes 12582912 | tf_op jit(solution)/shard_map/all_to_all | solution.py:206
  660.6 10.2 gather_fusion.3
  684.5 14.3 scatter_custom_fusion.4
  712.4 8.2 fusion.83
  720.6 62.3 %all-to-all-done.4 = bf16[8,384,1024]{2,1,0:T(8,128)(2,1)} async-done(((bf16[8,384,1024]{2,1,0:T(8,128)(2,1)}), bf16[8,384,1024]{2,1,0:T(8,128)(2,1)}, u32[]{:S(2)}, u32[]{:S(2)}) %all-to-all-start.4) | async-done | bytes 6291488 | tf_op jit(solution)/shard_map/all_to_all | solution.py:218
  782.9 8.9 bitcast_convert_fusion
  791.8 11.0 gather_fusion.4
  810.2 83.1 %all-reduce.10.cloned.1.call-done = bf16[1024,1024]{1,0:T(8,128)(2,1)} async-done(((bf16[1024,1024]{1,0:T(8,128)(2,1)}), bf16[1024,1024]{1,0:T(8,128)(2,1)}) %all-reduce.10.cloned.1.call-update) | async-done | bytes 2097168 | tf_op jit(solution)/shard_map/psum | solution.py:227
  907.0 144.0 %while.31 = (s32[]{:T(128)}, f32[1024,4,64]{0,2,1:T(8,128)S(1)}, f32[4,1024,4,64]{1,3,2,0:T(8,128)}, bf16[4,1024,4,64]{1,3,2,0:T(8,128)(2,1)}, bf16[4,1024,4,64]...) while((s32[]{:T(128)}, f32[1024,4,64]{0,2,1:T(8,128)S(1)}, ...), condition=%wide.region_30.31_spmd.clone, body=%wide.region_29.30_spmd.clone.sunk | while | flops 2728921088 | bytes 86579392 | solution.py:277
  909.6 9.2 fusion.220
  918.8 8.5 fusion.224
  927.3 9.4 fusion.221
  945.6 9.2 fusion.220
  954.7 8.5 fusion.224
  963.2 9.4 fusion.221
  981.5 9.2 fusion.220
  990.7 8.5 fusion.224
  999.2 9.4 fusion.221
  1017.5 9.2 fusion.220
  1026.6 8.5 fusion.224
  1035.1 9.4 fusion.221
  1085.2 14.1 reduce-scatter.12.cloned.1.call-done
  1099.3 38.2 %reduce-scatter.10.cloned.1.call-done = bf16[1024,256]{1,0:T(8,128)(2,1)} async-done(((bf16[4096,256]{1,0:T(8,128)(2,1)}), bf16[1024,256]{1,0:T(8,128)(2,1)}) %reduce-scatter.10.cloned.1.call-update) | async-done | bytes 524304 | tf_op jit(solution)/shard_map/reduce_scatter | solution.py:285
  1189.0 144.2 %all-reduce.12.cloned.1.call-done = (bf16[1024,1024]{1,0:T(8,128)(2,1)}, bf16[1024,1024]{1,0:T(8,128)(2,1)}) async-done(((bf16[1024,1024]{1,0:T(8,128)(2,1)}, bf16[1024,1024]{1,0:T(8,128)(2,1)}), (bf16[1024,1024]{1,0:T(8,128)(2,1)}, bf16[1024,1024]{1,0:T(8,128)(2,1)})) %all-reduce.12.cloned.1.call-update) | async-done | bytes 4194320 | tf_op jit(solution)/shard_map/psum | solution.py:192
  1336.7 14.7 all-reduce.2
  1359.8 27.3 %reduce-scatter.20.cloned.1.call-done = f32[1024,128]{1,0:T(8,128)} async-done(((f32[1024,1024]{1,0:T(8,128)}), f32[1024,128]{1,0:T(8,128)}) %reduce-scatter.20.cloned.1.call-update) | async-done | bytes 524304 | tf_op jit(solution)/shard_map/reduce_scatter | solution.py:309
  1387.0 55.1 %reduce-scatter.18.cloned.1.call-done = f32[128,1024]{1,0:T(8,128)} async-done(((f32[1024,1024]{1,0:T(8,128)}), f32[128,1024]{1,0:T(8,128)}) %reduce-scatter.18.cloned.1.call-update) | async-done | bytes 524304 | tf_op jit(solution)/shard_map/reduce_scatter | solution.py:308
  1442.2 39.6 %reduce-scatter.16.cloned.1.call-done = f32[256,128]{1,0:T(8,128)} async-done(((f32[256,1024]{1,0:T(8,128)}), f32[256,128]{1,0:T(8,128)}) %reduce-scatter.16.cloned.1.call-update) | async-done | bytes 131088 | tf_op jit(solution)/shard_map/reduce_scatter | solution.py:305
  1481.8 49.9 %reduce-scatter.14.cloned.1.call-done = f32[128,3,256]{2,0,1:T(8,128)} async-done(((f32[1024,3,256]{2,0,1:T(8,128)}), f32[128,3,256]{2,0,1:T(8,128)}) %reduce-scatter.14.cloned.1.call-update) | async-done | bytes 393232 | tf_op jit(solution)/shard_map/reduce_scatter | solution.py:304
  (317 shorter events, 342.7 us)
Async XLA Ops:
  7.2 398.9 %copy-start = (bf16[1,1024,1024]{2,1,0:T(8,128)(2,1)S(1)}, bf16[1,1024,1024]{2,1,0:T(8,128)(2,1)}, u32[]{:S(2)}) copy-start(bf16[1,1024,1024]{2,1,0:T(8,128)(2,1)} %param.30) | copy-start | bytes 6291460
  7.2 31.8 %all-gather.10.cloned.1.call-start = ((), (), s32[]{:S(2)}) async-start(), calls=%async_computation.12 | async-start | bytes 1769472 | tf_op jit(solution)/shard_map/all_gather | solution.py:61
  9.1 74.1 %all-gather.18.cloned.1.call-start = ((), (), s32[]{:S(2)}) async-start(), calls=%async_computation.24 | async-start | bytes 2621440 | tf_op jit(solution)/shard_map/all_gather | solution.py:80
  24.2 14.8 copy-start.40
  26.2 12.8 copy-start.33
  28.5 10.5 copy-start.42
  44.2 76.8 %all-gather.16.cloned.1.call-start = ((), (), s32[]{:S(2)}) async-start(), calls=%async_computation.23 | async-start | bytes 2621440 | tf_op jit(solution)/shard_map/all_gather | solution.py:79
  44.9 242.7 %all-reduce.8.cloned.1.call-start = ((), (), s32[]{:S(2)}) async-start(), calls=%async_computation.13 | async-start | bytes 4194304 | tf_op jit(solution)/shard_map/psum | solution.py:124
  69.4 129.0 %copy-start.14 = (bf16[256,1024]{1,0:T(8,128)(2,1)}, bf16[256,1024]{1,0:T(8,128)(2,1)S(1)}, u32[]{:S(2)}) copy-start(bf16[256,1024]{1,0:T(8,128)(2,1)S(1)} %all_gather.31) | copy-start | bytes 1572868
  196.9 13.1 copy-start.5
  196.9 93.8 %copy-start.23 = (f32[4,1024]{1,0:T(4,128)}, f32[4,1024]{1,0:T(4,128)S(1)}, u32[]{:S(2)}) copy-start(f32[4,1024]{1,0:T(4,128)S(1)} %get-tuple-element.138) | copy-start | bytes 49156
  196.9 93.8 %copy-start.25 = (f32[4,1024]{1,0:T(4,128)}, f32[4,1024]{1,0:T(4,128)S(1)}, u32[]{:S(2)}) copy-start(f32[4,1024]{1,0:T(4,128)S(1)} %get-tuple-element.136) | copy-start | bytes 49156
  196.9 93.8 %copy-start.27 = (s32[4,1024]{1,0:T(4,128)}, s32[4,1024]{1,0:T(4,128)S(1)}, u32[]{:S(2)}) copy-start(s32[4,1024]{1,0:T(4,128)S(1)} %get-tuple-element.679) | copy-start | bytes 49156
  196.9 16.4 %copy-start.53 = (bf16[128]{0:T(256)(128)(2,1)S(1)}, bf16[128]{0:T(256)(128)(2,1)}, u32[]{:S(2)}) copy-start(bf16[128]{0:T(256)(128)(2,1)} %param.25) | copy-start | bytes 772
  209.9 94.7 %all-to-all-start = ((s32[8,1,384]{2,1,0:T(1,128)}), s32[8,1,384]{2,1,0:T(1,128)S(1)}, u32[]{:S(2)}, u32[]{:S(2)}) async-start(s32[8,1,384]{2,1,0:T(1,128)} %bitcast.19), calls=%async_computation | async-start | bytes 24576 | tf_op jit(solution)/shard_map/all_to_all | solution.py:160
  227.8 64.2 %copy-start.44 = (f32[8,1,128]{2,1,0:T(1,128)}, f32[8,1,128]{2,1,0:T(1,128)S(1)}, u32[]{:S(2)}) copy-start(f32[8,1,128]{2,1,0:T(1,128)S(1)} %convert_element_type.206) | copy-start | bytes 12292
  304.6 84.1 %all-to-all-start.1 = ((bf16[8,384,1024]{2,1,0:T(8,128)(2,1)}), bf16[8,384,1024]{2,1,0:T(8,128)(2,1)}, u32[]{:S(2)}, u32[]{:S(2)}) async-start(bf16[8,384,1024]{2,1,0:T(8,128)(2,1)} %bitcast.321), calls=%async_computation.1 | async-start | bytes 12582912 | tf_op jit(solution)/shard_map/all_to_all | solution.py:157
  309.4 218.4 %all-gather.12.cloned.1.call-start = ((), (), s32[]{:S(2)}) async-start(), calls=%async_computation.14 | async-start | bytes 2359296 | tf_op jit(solution)/shard_map/all_gather | solution.py:65
  433.3 101.0 %all-to-all-start.2 = ((bf16[8,384,1024]{2,1,0:T(8,128)(2,1)}), bf16[8,384,1024]{2,1,0:T(8,128)(2,1)}, u32[]{:S(2)}, u32[]{:S(2)}) async-start(bf16[8,384,1024]{2,1,0:T(8,128)(2,1)} %bitcast.323), calls=%async_computation.2 | async-start | bytes 12582912 | tf_op jit(solution)/shard_map/all_to_all | solution.py:183
  438.3 115.8 %all-gather.14.cloned.1.call-start = ((), (), s32[]{:S(2)}) async-start(), calls=%async_computation.15 | async-start | bytes 2359296 | tf_op jit(solution)/shard_map/all_gather | solution.py:66
  525.4 374.7 %copy-start.30 = (f32[1024]{0:T(1024)}, f32[1024]{0:T(1024)S(1)}, u32[]{:S(2)}) copy-start(f32[1024]{0:T(1024)S(1)} %fusion.129) | copy-start | bytes 12292
  573.7 319.6 %copy-start.37 = (bf16[1024,2]{0,1:T(2,128)(2,1)}, bf16[1024,2]{0,1:T(2,128)(2,1)S(1)}, u32[]{:S(2)}) copy-start(bf16[1024,2]{0,1:T(2,128)(2,1)S(1)} %psum.38) | copy-start | bytes 12292
  573.8 319.5 %copy-start.28 = (f32[1024,2]{0,1:T(2,128)}, f32[1024,2]{0,1:T(2,128)S(1)}, u32[]{:S(2)}) copy-start(f32[1024,2]{0,1:T(2,128)S(1)} %get-tuple-element.357) | copy-start | bytes 24580
  573.8 319.5 %copy-start.50 = (f32[1024]{0:T(1024)}, f32[1024]{0:T(1024)S(1)}, u32[]{:S(2)}) copy-start(f32[1024]{0:T(1024)S(1)} %get-tuple-element.356) | copy-start | bytes 12292
  573.8 326.3 %copy-start.48 = (f32[1024,1]{0,1:T(1,128)}, f32[1024,1]{0,1:T(1,128)S(1)}, u32[]{:S(2)}) copy-start(f32[1024,1]{0,1:T(1,128)S(1)} %get-tuple-element.365) | copy-start | bytes 12292
  670.8 9.3 copy-start.55
  707.0 75.9 %all-to-all-start.4 = ((bf16[8,384,1024]{2,1,0:T(8,128)(2,1)}), bf16[8,384,1024]{2,1,0:T(8,128)(2,1)}, u32[]{:S(2)}, u32[]{:S(2)}) async-start(bf16[8,384,1024]{2,1,0:T(8,128)(2,1)} %bitcast.324), calls=%async_computation.4 | async-start | bytes 12582912 | tf_op jit(solution)/shard_map/all_to_all | solution.py:218
  711.9 181.4 %all-reduce.10.cloned.1.call-start = ((), (), s32[]{:S(2)}) async-start(), calls=%async_computation.16 | async-start | bytes 4194304 | tf_op jit(solution)/shard_map/psum | solution.py:227
  802.7 7.4 copy-start.24
  802.7 7.5 copy-start.26
  802.7 90.6 %copy-start.3 = (bf16[1,1024,1024]{2,1,0:T(8,128)(2,1)S(1)}, bf16[1,1024,1024]{2,1,0:T(8,128)(2,1)}, u32[]{:S(2)}) copy-start(bf16[1,1024,1024]{2,1,0:T(8,128)(2,1)} %param.18) | copy-start | bytes 6291460
  802.7 90.6 %copy-start.36 = (f32[1024]{0:T(1024)S(1)}, f32[1024]{0:T(1024)}, u32[]{:S(2)}) copy-start(f32[1024]{0:T(1024)} %copy-done.35) | copy-start | bytes 12292
  802.8 90.6 %copy-start.45 = (f32[8,1,128]{2,1,0:T(1,128)S(1)}, f32[8,1,128]{2,1,0:T(1,128)}, u32[]{:S(2)}) copy-start(f32[8,1,128]{2,1,0:T(1,128)} %copy-done.44) | copy-start | bytes 12292
  802.8 90.6 %copy-start.47 = (f32[1024]{0:T(1024)S(1)}, f32[1024]{0:T(1024)}, u32[]{:S(2)}) copy-start(f32[1024]{0:T(1024)} %copy-done.46) | copy-start | bytes 12292
  810.1 289.2 %reduce-scatter.12.cloned.1.call-start = ((), (), s32[]{:S(2)}) async-start(), calls=%async_computation.18 | async-start | bytes 2621440 | tf_op jit(solution)/shard_map/reduce_scatter | solution.py:288
  1064.9 72.6 %reduce-scatter.10.cloned.1.call-start = ((), (), s32[]{:S(2)}) async-start(), calls=%async_computation.17 | async-start | bytes 2621440 | tf_op jit(solution)/shard_map/reduce_scatter | solution.py:285
  1072.6 7.3 copy-start.51
  1079.8 95.3 %reduce-scatter.22.cloned.1.call-start = ((), (), s32[]{:S(2)}) async-start(), calls=%async_computation.25 | async-start | bytes 589824
  1083.0 250.2 %all-reduce.12.cloned.1.call-start = ((), (), s32[]{:S(2)}) async-start(), calls=%async_computation.26 | async-start | bytes 8388608 | tf_op jit(solution)/shard_map/psum | solution.py:192
  1142.4 244.7 %reduce-scatter.20.cloned.1.call-start = ((), (), s32[]{:S(2)}) async-start(), calls=%async_computation.22 | async-start | bytes 4718592 | tf_op jit(solution)/shard_map/reduce_scatter | solution.py:309
  1151.1 291.1 %reduce-scatter.18.cloned.1.call-start = ((), (), s32[]{:S(2)}) async-start(), calls=%async_computation.21 | async-start | bytes 4718592 | tf_op jit(solution)/shard_map/reduce_scatter | solution.py:308
  1157.2 324.6 %reduce-scatter.16.cloned.1.call-start = ((), (), s32[]{:S(2)}) async-start(), calls=%async_computation.20 | async-start | bytes 1179648 | tf_op jit(solution)/shard_map/reduce_scatter | solution.py:305
  1162.1 369.6 %reduce-scatter.14.cloned.1.call-start = ((), (), s32[]{:S(2)}) async-start(), calls=%async_computation.19 | async-start | bytes 3538944 | tf_op jit(solution)/shard_map/reduce_scatter | solution.py:304
  1167.4 16.8 %slice-start = ((s8[4718592]{0:T(1024)(128)(4,1)}), s8[524288]{0:T(1024)(128)(4,1)S(1)}, s32[]{:S(2)}) async-start(s8[4718592]{0:T(1024)(128)(4,1)} %bitcast.359), calls=%async_computation.27 | async-start | bytes 1048576
  1176.6 7.6 copy-start.22
  1176.6 7.6 slice-start.1
  1189.0 147.7 %copy-start.52 = (f32[1024]{0:T(1024)S(1)}, f32[1024]{0:T(1024)}, u32[]{:S(2)}) copy-start(f32[1024]{0:T(1024)} %get-tuple-element.292) | copy-start | bytes 12292
  1352.6 179.1 %copy-start.1 = (bf16[1,1024,1024]{2,1,0:T(8,128)(2,1)S(1)}, bf16[1,1024,1024]{2,1,0:T(8,128)(2,1)}, u32[]{:S(2)}) copy-start(bf16[1,1024,1024]{2,1,0:T(8,128)(2,1)} %param.30) | copy-start | bytes 6291460
  (38 other events, 145.6 us)
Sparse Core Ops, SparseCore 0:
  10.5 28.4 all-gather.9
  44.3 38.9 all-gather.17
  85.7 35.1 all-gather.15
  201.4 86.1 all-reduce.7
  311.7 59.7 all-gather.11
  440.7 60.1 all-gather.13
  810.2 83.0 all-reduce.9
  1065.1 34.2 reduce-scatter.11
  1102.3 35.1 reduce-scatter.9
  1141.0 34.1 reduce-scatter.21
  1178.2 155.0 all-reduce.11
  1337.0 50.0 reduce-scatter.19
  1391.0 51.1 reduce-scatter.17
  1445.8 35.9 reduce-scatter.15
  1485.6 46.0 reduce-scatter.13
where the time goes:
time: 1540 us
  waiting for transfers between devices  702 us (46%)
  matrix products  287 us (19%)
  blocking collectives  242 us (16%)
  local copies, waits for them, and re-layouts  155 us (10%)
  other arithmetic  116 us (8%)
  starting transfers between devices  19.9 us (1%)
  between operations  16.5 us (1%)
    psum x1, waiting for transfers between devices, local(): mixed = lax.psum(mixed_part.astype(jnp.bfloat16), 'tp').astype(jnp.float32)  144 us
    all_gather x1, blocking collectives, local(): lax.all_gather(mix_weight, ('shard', 'ctx'), axis=0, tiled=True)  86.6 us
    psum x1, waiting for transfers between devices, local(): lax.psum((normed2_part + expert_tok_grad).astype(jnp.bfloat16), 'tp')  83.1 us
    all_to_all x1, blocking collectives, local(): lax.all_to_all(pack_rows(expert_grad), ('shard', 'ctx'), split_axis=0, co...  76.7 us
    all_to_all x1, waiting for transfers between devices, local(): lax.all_to_all(pack_rows(normed2_low), ('shard', 'ctx'), split_axis=0, co...  66.5 us
    all_to_all x1, waiting for transfers between devices, local(): lax.all_to_all(unfold_rows(expert_in_grad).astype(jnp.bfloat16), ('shard'...  62.3 us
    psum x1, waiting for transfers between devices, local(): lax.psum(branch_part.astype(jnp.bfloat16), 'tp').astype(jnp.float32)  59.8 us
    reduce_scatter x1, waiting for transfers between devices, local(): lax.psum_scatter(up_grad, ('shard', 'ctx'), scatter_dimension=0, tiled=True)  55.1 us
  transfers between devices with their start and end apart: 19, of which 15 were waited for; matrix products, arithmetic and copies ran while one was open for 13% of the time, Pallas kernels for 0%

commit v1 on v0

--- a/solution.py
+++ b/solution.py
@@ -224,7 +224,9 @@
     ).astype(jnp.float32)
     expert_tok_grad = sent_back.reshape(-1, model_width)[full_index] * live_rows
     normed2_grad, branch_dots = (
-        lax.psum((normed2_part + expert_tok_grad).astype(jnp.bfloat16), "tp").astype(jnp.float32),
+        jnp.sum(
+            lax.all_gather((normed2_part + expert_tok_grad).astype(jnp.bfloat16), "tp"), axis=0
+        ).astype(jnp.float32),
         lax.psum(dots_part.astype(jnp.bfloat16), "tp").astype(jnp.float32),
     )
     logit_grad = mixing * (branch_dots - jnp.sum(mixing * branch_dots, axis=-1, keepdims=True))

time: 1540 us -> 1610 us (1.045)
  waiting for transfers between devices: 702 us -> 764 us
    all_gather x0 -> x1, waiting for transfers between devices: none -> 147 us  [local(): lax.all_gather((normed2_part + expert_tok_grad).astype(jnp.bfloat16), 'tp')]
    psum x1 -> x0, waiting for transfers between devices: 83.1 us -> none  [local(): lax.psum((normed2_part + expert_tok_grad).astype(jnp.bfloat16), 'tp')]
where the time goes in v1:
time: 1610 us
  waiting for transfers between devices  764 us (47%)
  matrix products  286 us (18%)
  blocking collectives  242 us (15%)
  local copies, waits for them, and re-layouts  155 us (10%)
  other arithmetic  124 us (8%)
  starting transfers between devices  19.7 us (1%)
  between operations  16.5 us (1%)
    all_gather x1, waiting for transfers between devices, local(): lax.all_gather((normed2_part + expert_tok_grad).astype(jnp.bfloat16), 'tp')  147 us
    psum x1, waiting for transfers between devices, local(): mixed = lax.psum(mixed_part.astype(jnp.bfloat16), 'tp').astype(jnp.float32)  144 us
    all_gather x1, blocking collectives, local(): lax.all_gather(mix_weight, ('shard', 'ctx'), axis=0, tiled=True)  86.6 us
    all_to_all x1, blocking collectives, local(): lax.all_to_all(pack_rows(expert_grad), ('shard', 'ctx'), split_axis=0, co...  76.7 us
    all_to_all x1, waiting for transfers between devices, local(): lax.all_to_all(pack_rows(normed2_low), ('shard', 'ctx'), split_axis=0, co...  66.5 us
    all_to_all x1, waiting for transfers between devices, local(): lax.all_to_all(unfold_rows(expert_in_grad).astype(jnp.bfloat16), ('shard'...  62.3 us
    psum x1, waiting for transfers between devices, local(): lax.psum(branch_part.astype(jnp.bfloat16), 'tp').astype(jnp.float32)  59.9 us
    reduce_scatter x1, waiting for transfers between devices, local(): lax.psum_scatter(up_grad, ('shard', 'ctx'), scatter_dimension=0, tiled=True)  55.1 us
  transfers between devices with their start and end apart: 19, of which 15 were waited for; matrix products, arithmetic and copies ran while one was open for 13% of the time, Pallas kernels for 0%

profile of v1, /device:TPU:0, one launch (start us, length us, event | category | flops | bytes accessed | tf_op | source)
XLA Modules:
  0.0 1608.7 jit_solution(11637996669362147959)
XLA Ops:
  9.2 15.0 all-gather.3
  28.5 10.5 all-gather.12.cloned.1.call-done
  45.0 24.8 %all_gather.37 = bf16[256,1024]{1,0:T(8,128)(2,1)S(1)} all-gather(bf16[256,128]{1,0:T(8,128)(2,1)S(1)} %copy-done.32), channel_id=1, replica_groups=mesh['shard'=2,'ctx'=4,'tp'=4] {'shard','ctx'}, dimensions={1}, use_global_device_ids=true | all-gather | bytes 589824 | tf_op jit(solution)/shard_map/all_gather | solution.py:62
  69.8 13.2 all-gather.20.cloned.1.call-done
  90.9 29.6 %all-gather.18.cloned.1.call-done = bf16[4096,1,256]{0,2,1:T(8,128)(2,1)} async-done(((bf16[1024,1,256]{0,2,1:T(8,128)(2,1)}), bf16[4096,1,256]{0,2,1:T(8,128)(2,1)}) %all-gather.18.cloned.1.call-update) | async-done | bytes 2097168 | tf_op jit(solution)/shard_map/all_gather | solution.py:79
  128.6 67.9 %while.30 = (s32[]{:T(128)}, f32[4,1024]{1,0:T(4,128)S(1)}, f32[4,1024]{1,0:T(4,128)S(1)}, f32[4,1024,64]{1,2,0:T(8,128)}, s32[4,1024]{1,0:T(4,128)S(1)}, /*inde...) while((s32[]{:T(128)}, f32[4,1024]{1,0:T(4,128)S(1)}, ...), condition=%wide.region_5.6_spmd.clone, body=%wide.region_2.5_spmd.clone.sunk | while | flops 1131173888 | bytes 66869456 | solution.py:117
  212.9 14.5 all-gather.4
  227.4 59.9 %all-reduce.7.cloned.1.call-done = bf16[1024,1024]{1,0:T(8,128)(2,1)} async-done(((bf16[1024,1024]{1,0:T(8,128)(2,1)}), bf16[1024,1024]{1,0:T(8,128)(2,1)}) %all-reduce.7.cloned.1.call-update) | async-done | bytes 2097168 | tf_op jit(solution)/shard_map/psum | solution.py:124
  294.5 9.8 scatter_custom_fusion.1
  321.9 66.5 %all-to-all-done.1 = bf16[8,384,1024]{2,1,0:T(8,128)(2,1)} async-done(((bf16[8,384,1024]{2,1,0:T(8,128)(2,1)}), bf16[8,384,1024]{2,1,0:T(8,128)(2,1)}, u32[]{:S(2)}, u32[]{:S(2)}) %all-to-all-start.1) | async-done | bytes 6291488 | tf_op jit(solution)/shard_map/all_to_all | solution.py:157
  388.4 10.2 gather_fusion
  410.3 14.8 scatter_custom_fusion.2
  425.1 8.2 convert_element_type.177
  438.8 86.6 %all_gather.39 = bf16[1024,2]{0,1:T(2,128)(2,1)S(1)} all-gather(bf16[128,2]{0,1:T(2,128)(2,1)S(1)} %copy-done.54), channel_id=1, replica_groups=mesh['shard'=2,'ctx'=4,'tp'=4] {'shard','ctx'}, dimensions={0}, use_global_device_ids=true | all-gather | bytes 4608 | tf_op jit(solution)/shard_map/all_gather | solution.py:64
  534.3 8.9 bitcast_convert_fusion.1
  543.2 10.9 gather_fusion.2
  554.1 9.6 fusion.91
  563.7 10.0 psum.30
  573.8 10.1 scatter_custom_fusion.3
  583.8 76.7 %all_to_all.29 = bf16[8,384,1024]{2,1,0:T(8,128)(2,1)} all-to-all(bf16[8,384,1024]{2,1,0:T(8,128)(2,1)} %bitcast.323), channel_id=1, replica_groups=mesh['shard'=2,'ctx'=4,'tp'=4] {'shard','ctx'}, dimensions={0} | all-to-all | bytes 12582912 | tf_op jit(solution)/shard_map/all_to_all | solution.py:206
  660.5 10.2 gather_fusion.3
  684.4 14.3 scatter_custom_fusion.4
  712.3 8.2 fusion.83
  720.5 62.3 %all-to-all-done.4 = bf16[8,384,1024]{2,1,0:T(8,128)(2,1)} async-done(((bf16[8,384,1024]{2,1,0:T(8,128)(2,1)}), bf16[8,384,1024]{2,1,0:T(8,128)(2,1)}, u32[]{:S(2)}, u32[]{:S(2)}) %all-to-all-start.4) | async-done | bytes 6291488 | tf_op jit(solution)/shard_map/all_to_all | solution.py:218
  782.8 8.9 bitcast_convert_fusion
  791.7 11.0 gather_fusion.4
  810.0 146.6 %all-gather.22.cloned.1.call-done = bf16[4096,1024]{1,0:T(8,128)(2,1)} async-done(((bf16[1024,1024]{1,0:T(8,128)(2,1)}), bf16[4096,1024]{1,0:T(8,128)(2,1)}) %all-gather.22.cloned.1.call-update) | async-done | bytes 8388624 | tf_op jit(solution)/shard_map/all_gather | solution.py:228
  977.9 144.0 %while.31 = (s32[]{:T(128)}, f32[1024,4,64]{0,2,1:T(8,128)S(1)}, f32[4,1024,4,64]{1,3,2,0:T(8,128)}, bf16[4,1024,4,64]{1,3,2,0:T(8,128)(2,1)}, bf16[4,1024,4,64]...) while((s32[]{:T(128)}, f32[1024,4,64]{0,2,1:T(8,128)S(1)}, ...), condition=%wide.region_30.31_spmd.clone, body=%wide.region_29.30_spmd.clone.sunk | while | flops 2728921088 | bytes 86579392 | solution.py:279
  980.5 9.2 fusion.220
  989.7 8.5 fusion.224
  998.2 9.4 fusion.221
  1016.5 9.2 fusion.220
  1025.6 8.5 fusion.224
  1034.1 9.4 fusion.221
  1052.4 9.2 fusion.220
  1061.6 8.5 fusion.224
  1070.1 9.4 fusion.221
  1088.4 9.2 fusion.220
  1097.5 8.5 fusion.224
  1106.0 9.4 fusion.221
  1156.1 13.2 reduce-scatter.12.cloned.1.call-done
  1169.4 38.2 %reduce-scatter.10.cloned.1.call-done = bf16[1024,256]{1,0:T(8,128)(2,1)} async-done(((bf16[4096,256]{1,0:T(8,128)(2,1)}), bf16[1024,256]{1,0:T(8,128)(2,1)}) %reduce-scatter.10.cloned.1.call-update) | async-done | bytes 524304 | tf_op jit(solution)/shard_map/reduce_scatter | solution.py:287
  1259.0 144.2 %all-reduce.9.cloned.1.call-done = (bf16[1024,1024]{1,0:T(8,128)(2,1)}, bf16[1024,1024]{1,0:T(8,128)(2,1)}) async-done(((bf16[1024,1024]{1,0:T(8,128)(2,1)}, bf16[1024,1024]{1,0:T(8,128)(2,1)}), (bf16[1024,1024]{1,0:T(8,128)(2,1)}, bf16[1024,1024]{1,0:T(8,128)(2,1)})) %all-reduce.9.cloned.1.call-update) | async-done | bytes 4194320 | tf_op jit(solution)/shard_map/psum | solution.py:192
  1406.8 14.7 all-reduce.2
  1429.8 27.3 %reduce-scatter.20.cloned.1.call-done = f32[1024,128]{1,0:T(8,128)} async-done(((f32[1024,1024]{1,0:T(8,128)}), f32[1024,128]{1,0:T(8,128)}) %reduce-scatter.20.cloned.1.call-update) | async-done | bytes 524304 | tf_op jit(solution)/shard_map/reduce_scatter | solution.py:311
  1457.1 55.1 %reduce-scatter.18.cloned.1.call-done = f32[128,1024]{1,0:T(8,128)} async-done(((f32[1024,1024]{1,0:T(8,128)}), f32[128,1024]{1,0:T(8,128)}) %reduce-scatter.18.cloned.1.call-update) | async-done | bytes 524304 | tf_op jit(solution)/shard_map/reduce_scatter | solution.py:310
  1512.2 39.6 %reduce-scatter.16.cloned.1.call-done = f32[256,128]{1,0:T(8,128)} async-done(((f32[256,1024]{1,0:T(8,128)}), f32[256,128]{1,0:T(8,128)}) %reduce-scatter.16.cloned.1.call-update) | async-done | bytes 131088 | tf_op jit(solution)/shard_map/reduce_scatter | solution.py:307
  1551.8 49.9 %reduce-scatter.14.cloned.1.call-done = f32[128,3,256]{2,0,1:T(8,128)} async-done(((f32[1024,3,256]{2,0,1:T(8,128)}), f32[128,3,256]{2,0,1:T(8,128)}) %reduce-scatter.14.cloned.1.call-update) | async-done | bytes 393232 | tf_op jit(solution)/shard_map/reduce_scatter | solution.py:306
  (318 shorter events, 350.2 us)
Async XLA Ops:
  7.2 398.5 %copy-start = (bf16[1,1024,1024]{2,1,0:T(8,128)(2,1)S(1)}, bf16[1,1024,1024]{2,1,0:T(8,128)(2,1)}, u32[]{:S(2)}) copy-start(bf16[1,1024,1024]{2,1,0:T(8,128)(2,1)} %param.30) | copy-start | bytes 6291460
  7.2 31.8 %all-gather.12.cloned.1.call-start = ((), (), s32[]{:S(2)}) async-start(), calls=%async_computation.12 | async-start | bytes 1769472 | tf_op jit(solution)/shard_map/all_gather | solution.py:61
  9.1 73.8 %all-gather.20.cloned.1.call-start = ((), (), s32[]{:S(2)}) async-start(), calls=%async_computation.23 | async-start | bytes 2621440 | tf_op jit(solution)/shard_map/all_gather | solution.py:80
  24.2 14.8 copy-start.40
  26.2 12.8 copy-start.33
  28.5 10.5 copy-start.42
  44.2 76.4 %all-gather.18.cloned.1.call-start = ((), (), s32[]{:S(2)}) async-start(), calls=%async_computation.22 | async-start | bytes 2621440 | tf_op jit(solution)/shard_map/all_gather | solution.py:79
  44.9 242.4 %all-reduce.7.cloned.1.call-start = ((), (), s32[]{:S(2)}) async-start(), calls=%async_computation.13 | async-start | bytes 4194304 | tf_op jit(solution)/shard_map/psum | solution.py:124
  69.8 128.3 %copy-start.14 = (bf16[256,1024]{1,0:T(8,128)(2,1)}, bf16[256,1024]{1,0:T(8,128)(2,1)S(1)}, u32[]{:S(2)}) copy-start(bf16[256,1024]{1,0:T(8,128)(2,1)S(1)} %all_gather.37) | copy-start | bytes 1572868
  196.5 13.1 copy-start.5
  196.5 93.8 %copy-start.23 = (f32[4,1024]{1,0:T(4,128)}, f32[4,1024]{1,0:T(4,128)S(1)}, u32[]{:S(2)}) copy-start(f32[4,1024]{1,0:T(4,128)S(1)} %get-tuple-element.138) | copy-start | bytes 49156
  196.5 93.8 %copy-start.25 = (f32[4,1024]{1,0:T(4,128)}, f32[4,1024]{1,0:T(4,128)S(1)}, u32[]{:S(2)}) copy-start(f32[4,1024]{1,0:T(4,128)S(1)} %get-tuple-element.136) | copy-start | bytes 49156
  196.5 93.8 %copy-start.27 = (s32[4,1024]{1,0:T(4,128)}, s32[4,1024]{1,0:T(4,128)S(1)}, u32[]{:S(2)}) copy-start(s32[4,1024]{1,0:T(4,128)S(1)} %get-tuple-element.680) | copy-start | bytes 49156
  196.5 16.4 %copy-start.53 = (bf16[128]{0:T(256)(128)(2,1)S(1)}, bf16[128]{0:T(256)(128)(2,1)}, u32[]{:S(2)}) copy-start(bf16[128]{0:T(256)(128)(2,1)} %param.25) | copy-start | bytes 772
  209.6 94.7 %all-to-all-start = ((s32[8,1,384]{2,1,0:T(1,128)}), s32[8,1,384]{2,1,0:T(1,128)S(1)}, u32[]{:S(2)}, u32[]{:S(2)}) async-start(s32[8,1,384]{2,1,0:T(1,128)} %bitcast.19), calls=%async_computation | async-start | bytes 24576 | tf_op jit(solution)/shard_map/all_to_all | solution.py:160
  227.4 64.3 %copy-start.44 = (f32[8,1,128]{2,1,0:T(1,128)}, f32[8,1,128]{2,1,0:T(1,128)S(1)}, u32[]{:S(2)}) copy-start(f32[8,1,128]{2,1,0:T(1,128)S(1)} %convert_element_type.208) | copy-start | bytes 12292
  304.3 84.1 %all-to-all-start.1 = ((bf16[8,384,1024]{2,1,0:T(8,128)(2,1)}), bf16[8,384,1024]{2,1,0:T(8,128)(2,1)}, u32[]{:S(2)}, u32[]{:S(2)}) async-start(bf16[8,384,1024]{2,1,0:T(8,128)(2,1)} %bitcast.322), calls=%async_computation.1 | async-start | bytes 12582912 | tf_op jit(solution)/shard_map/all_to_all | solution.py:157
  309.0 218.7 %all-gather.14.cloned.1.call-start = ((), (), s32[]{:S(2)}) async-start(), calls=%async_computation.14 | async-start | bytes 2359296 | tf_op jit(solution)/shard_map/all_gather | solution.py:65
  433.3 101.0 %all-to-all-start.2 = ((bf16[8,384,1024]{2,1,0:T(8,128)(2,1)}), bf16[8,384,1024]{2,1,0:T(8,128)(2,1)}, u32[]{:S(2)}, u32[]{:S(2)}) async-start(bf16[8,384,1024]{2,1,0:T(8,128)(2,1)} %bitcast.324), calls=%async_computation.2 | async-start | bytes 12582912 | tf_op jit(solution)/shard_map/all_to_all | solution.py:183
  438.2 115.8 %all-gather.16.cloned.1.call-start = ((), (), s32[]{:S(2)}) async-start(), calls=%async_computation.15 | async-start | bytes 2359296 | tf_op jit(solution)/shard_map/all_gather | solution.py:66
  525.4 445.6 %copy-start.30 = (f32[1024]{0:T(1024)}, f32[1024]{0:T(1024)S(1)}, u32[]{:S(2)}) copy-start(f32[1024]{0:T(1024)S(1)} %fusion.129) | copy-start | bytes 12292
  573.7 390.5 %copy-start.37 = (bf16[1024,2]{0,1:T(2,128)(2,1)}, bf16[1024,2]{0,1:T(2,128)(2,1)S(1)}, u32[]{:S(2)}) copy-start(bf16[1024,2]{0,1:T(2,128)(2,1)S(1)} %psum.30) | copy-start | bytes 12292
  573.7 390.5 %copy-start.28 = (f32[1024,2]{0,1:T(2,128)}, f32[1024,2]{0,1:T(2,128)S(1)}, u32[]{:S(2)}) copy-start(f32[1024,2]{0,1:T(2,128)S(1)} %get-tuple-element.357) | copy-start | bytes 24580
  573.7 390.5 %copy-start.50 = (f32[1024]{0:T(1024)}, f32[1024]{0:T(1024)S(1)}, u32[]{:S(2)}) copy-start(f32[1024]{0:T(1024)S(1)} %get-tuple-element.356) | copy-start | bytes 12292
  573.8 397.2 %copy-start.48 = (f32[1024,1]{0,1:T(1,128)}, f32[1024,1]{0,1:T(1,128)S(1)}, u32[]{:S(2)}) copy-start(f32[1024,1]{0,1:T(1,128)S(1)} %get-tuple-element.365) | copy-start | bytes 12292
  670.7 9.3 copy-start.55
  706.9 75.9 %all-to-all-start.4 = ((bf16[8,384,1024]{2,1,0:T(8,128)(2,1)}), bf16[8,384,1024]{2,1,0:T(8,128)(2,1)}, u32[]{:S(2)}, u32[]{:S(2)}) async-start(bf16[8,384,1024]{2,1,0:T(8,128)(2,1)} %bitcast.325), calls=%async_computation.4 | async-start | bytes 12582912 | tf_op jit(solution)/shard_map/all_to_all | solution.py:218
  711.8 244.7 %all-gather.22.cloned.1.call-start = ((), (), s32[]{:S(2)}) async-start(), calls=%async_computation.24 | async-start | bytes 10485760 | tf_op jit(solution)/shard_map/all_gather | solution.py:228
  802.7 7.3 copy-start.24
  802.7 7.3 copy-start.26
  809.9 359.5 %reduce-scatter.12.cloned.1.call-start = ((), (), s32[]{:S(2)}) async-start(), calls=%async_computation.17 | async-start | bytes 2621440 | tf_op jit(solution)/shard_map/reduce_scatter | solution.py:290
  956.6 7.6 copy-start.3
  956.6 7.6 copy-start.36
  956.6 7.6 copy-start.45
  956.6 7.7 copy-start.47
  1135.8 71.7 %reduce-scatter.10.cloned.1.call-start = ((), (), s32[]{:S(2)}) async-start(), calls=%async_computation.16 | async-start | bytes 2621440 | tf_op jit(solution)/shard_map/reduce_scatter | solution.py:287
  1143.5 7.3 copy-start.51
  1150.7 94.5 %reduce-scatter.22.cloned.1.call-start = ((), (), s32[]{:S(2)}) async-start(), calls=%async_computation.25 | async-start | bytes 589824
  1153.9 249.3 %all-reduce.9.cloned.1.call-start = ((), (), s32[]{:S(2)}) async-start(), calls=%async_computation.26 | async-start | bytes 8388608 | tf_op jit(solution)/shard_map/psum | solution.py:192
  1212.4 244.7 %reduce-scatter.20.cloned.1.call-start = ((), (), s32[]{:S(2)}) async-start(), calls=%async_computation.21 | async-start | bytes 4718592 | tf_op jit(solution)/shard_map/reduce_scatter | solution.py:311
  1221.1 291.1 %reduce-scatter.18.cloned.1.call-start = ((), (), s32[]{:S(2)}) async-start(), calls=%async_computation.20 | async-start | bytes 4718592 | tf_op jit(solution)/shard_map/reduce_scatter | solution.py:310
  1227.2 324.6 %reduce-scatter.16.cloned.1.call-start = ((), (), s32[]{:S(2)}) async-start(), calls=%async_computation.19 | async-start | bytes 1179648 | tf_op jit(solution)/shard_map/reduce_scatter | solution.py:307
  1232.1 369.5 %reduce-scatter.14.cloned.1.call-start = ((), (), s32[]{:S(2)}) async-start(), calls=%async_computation.18 | async-start | bytes 3538944 | tf_op jit(solution)/shard_map/reduce_scatter | solution.py:306
  1237.5 16.8 %slice-start = ((s8[4718592]{0:T(1024)(128)(4,1)}), s8[524288]{0:T(1024)(128)(4,1)S(1)}, s32[]{:S(2)}) async-start(s8[4718592]{0:T(1024)(128)(4,1)} %bitcast.361), calls=%async_computation.27 | async-start | bytes 1048576
  1246.7 7.6 copy-start.22
  1246.7 7.6 slice-start.1
  1259.0 147.7 %copy-start.52 = (f32[1024]{0:T(1024)S(1)}, f32[1024]{0:T(1024)}, u32[]{:S(2)}) copy-start(f32[1024]{0:T(1024)} %get-tuple-element.292) | copy-start | bytes 12292
  1422.6 179.1 %copy-start.1 = (bf16[1,1024,1024]{2,1,0:T(8,128)(2,1)S(1)}, bf16[1,1024,1024]{2,1,0:T(8,128)(2,1)}, u32[]{:S(2)}) copy-start(bf16[1,1024,1024]{2,1,0:T(8,128)(2,1)} %param.30) | copy-start | bytes 6291460
  (38 other events, 145.6 us)
Sparse Core Ops, SparseCore 0:
  10.5 28.4 all-gather.11
  44.3 38.6 all-gather.19
  85.4 35.1 all-gather.17
  201.1 86.1 all-reduce.6
  311.4 59.7 all-gather.13
  440.6 60.1 all-gather.15
  810.0 146.5 all-gather.21
  1135.9 33.3 reduce-scatter.11
  1172.3 35.1 reduce-scatter.9
  1211.1 34.1 reduce-scatter.21
  1248.2 154.9 all-reduce.8
  1407.0 50.0 reduce-scatter.19
  1461.0 51.1 reduce-scatter.17
  1515.8 35.9 reduce-scatter.15
  1555.6 46.0 reduce-scatter.13
